TPU v7x, 32 devices: a whole 2x2x4 slice. The times are simulated.
32 devices in a mesh: row: 4 (over y, x), col: 8 (over z, core).
Axes of the slice: x: 2, y: 2, z: 4, core: 2. Of those that a mesh axis runs over, the one named last changes fastest.
Arguments:
- e_field: float32 [3, 64, 32, 1024], P(None, None, 'row', 'col'), may hold values from -6 to 6
- h_field: float32 [3, 64, 32, 1024], P(None, None, 'row', 'col'), may hold values from -6 to 6
- e_coef: float32 [64, 32, 1024], P(None, 'row', 'col'), may hold values from 0.125 to 0.5
- basis: float32 [128, 32, 1024], P('row', None, 'col'), may hold values from -0.03125 to 0.03125
- pml_width: int32 [4], replicated, may hold values from 2 to 8
- snap_index: int32 [64], replicated, may hold values from 0 to 383
Outputs:
- e_final: float32 [3, 64, 32, 1024], P(None, None, 'row', 'col')
- h_final: float32 [3, 64, 32, 1024], P(None, None, 'row', 'col')
- coefficients: float32 [64, 128], replicated
- gram: float32 [64, 64], replicated
All inputs are finite; a program needn't handle non-finite values.
Results may differ from a plain program's by a relative error of at most 0.00008.
Values sent between devices are 32-bit elements; how exact they have to be, the bound alone decides.
A program may use at most 64 MiB of HBM per device.

v0:
```python
import jax
import jax.numpy as jnp
from jax import lax
from jax.sharding import PartitionSpec as P

STEPS = 8


time_step = 0.5
sigma_top = 4.0
alpha_shift = 0.05


def from_behind(block, axis, distance):
    devices = range(lax.axis_size(axis))
    route = [(i - distance, i) for i in devices if i - distance in devices]
    return lax.ppermute(block, axis, route)


def forward(field, axis, plane):
    count = field.shape[axis]
    after = jnp.concatenate(
        [lax.slice_in_dim(field, 1, count, axis=axis), jnp.expand_dims(plane, axis)], axis
    )
    return after - field


def backward(field, axis, plane):
    count = field.shape[axis]
    before = jnp.concatenate(
        [jnp.expand_dims(plane, axis), lax.slice_in_dim(field, 0, count - 1, axis=axis)], axis
    )
    return field - before


def absorber(positions, total, low, high):
    depth = jnp.maximum(
        jnp.maximum((low - positions) / low, (positions - (total - 1.0 - high)) / high), 0.0
    )
    sigma = sigma_top * depth**3
    damp = jnp.exp(-(sigma + alpha_shift) * time_step)
    gain = sigma / (sigma + alpha_shift) * (damp - 1.0)
    return (damp, gain)


def magnetic(e_field, h_field, psi, next_x, next_y, damp_x, gain_x, damp_y, gain_y):
    e_x, e_y, e_z = (e_field[0], e_field[1], e_field[2])
    h_x, h_y, h_z = (h_field[0], h_field[1], h_field[2])
    zplane = jnp.zeros_like(e_x[0])
    ez_dy = forward(e_z, 2, next_y[1])
    ey_dz = forward(e_y, 0, zplane)
    ex_dz = forward(e_x, 0, zplane)
    ez_dx = forward(e_z, 1, next_x[1])
    ey_dx = forward(e_y, 1, next_x[0])
    ex_dy = forward(e_x, 2, next_y[0])
    psi_hxy = damp_y * psi[0] + gain_y * ez_dy
    psi_hyx = damp_x * psi[1] + gain_x * ez_dx
    psi_hzx = damp_x * psi[2] + gain_x * ey_dx
    psi_hzy = damp_y * psi[3] + gain_y * ex_dy
    h_x = h_x - time_step * (ez_dy + psi_hxy - ey_dz)
    h_y = h_y - time_step * (ex_dz - ez_dx - psi_hyx)
    h_z = h_z - time_step * (ey_dx + psi_hzx - ex_dy - psi_hzy)
    return (jnp.stack((h_x, h_y, h_z)), (psi_hxy, psi_hyx, psi_hzx, psi_hzy))


def electric(e_field, h_field, psi, e_coef, prev_x, prev_y, damp_x, gain_x, damp_y, gain_y):
    e_x, e_y, e_z = (e_field[0], e_field[1], e_field[2])
    h_x, h_y, h_z = (h_field[0], h_field[1], h_field[2])
    zplane = jnp.zeros_like(h_x[0])
    hz_dy = backward(h_z, 2, prev_y[1])
    hy_dz = backward(h_y, 0, zplane)
    hx_dz = backward(h_x, 0, zplane)
    hz_dx = backward(h_z, 1, prev_x[1])
    hy_dx = backward(h_y, 1, prev_x[0])
    hx_dy = backward(h_x, 2, prev_y[0])
    psi_exy = damp_y * psi[0] + gain_y * hz_dy
    psi_eyx = damp_x * psi[1] + gain_x * hz_dx
    psi_ezx = damp_x * psi[2] + gain_x * hy_dx
    psi_ezy = damp_y * psi[3] + gain_y * hx_dy
    e_x = e_x + e_coef * (hz_dy + psi_exy - hy_dz)
    e_y = e_y + e_coef * (hx_dz - hz_dx - psi_eyx)
    e_z = e_z + e_coef * (hy_dx + psi_ezx - hx_dy - psi_ezy)
    return (jnp.stack((e_x, e_y, e_z)), (psi_exy, psi_eyx, psi_ezx, psi_ezy))


def shards(e_field, h_field, e_coef, basis, pml_width, snap_index):
    depth_z, rows_here, cols_here = e_coef.shape
    full_x = rows_here * lax.axis_size("row")
    full_y = cols_here * lax.axis_size("col")
    x_first = lax.axis_index("row") * rows_here
    y_first = lax.axis_index("col") * cols_here
    widths = pml_width.astype(jnp.float32)
    x_pos = x_first.astype(jnp.float32) + jnp.arange(rows_here, dtype=jnp.float32)
    y_pos = y_first.astype(jnp.float32) + jnp.arange(cols_here, dtype=jnp.float32)
    hdx, hgx = absorber(x_pos + 0.5, float(full_x), widths[0], widths[1])
    hdy, hgy = absorber(y_pos + 0.5, float(full_y), widths[2], widths[3])
    edx, egx = absorber(x_pos, float(full_x), widths[0], widths[1])
    edy, egy = absorber(y_pos, float(full_y), widths[2], widths[3])
    hdx, hgx, edx, egx = [v.reshape(1, rows_here, 1) for v in (hdx, hgx, edx, egx)]
    hdy, hgy, edy, egy = [v.reshape(1, 1, cols_here) for v in (hdy, hgy, edy, egy)]
    zeros_cells = jnp.zeros((depth_z, rows_here, cols_here), jnp.float32)
    psi_mag = (zeros_cells,) * 4
    psi_ele = (zeros_cells,) * 4
    for step in range(STEPS):
        next_x = from_behind(e_field[1:3, :, 0, :], "row", -1)
        next_y = from_behind(jnp.stack((e_field[0, :, :, 0], e_field[2, :, :, 0])), "col", -1)
        h_field, psi_mag = magnetic(e_field, h_field, psi_mag, next_x, next_y, hdx, hgx, hdy, hgy)
        prev_x = from_behind(h_field[1:3, :, -1, :], "row", 1)
        prev_y = from_behind(jnp.stack((h_field[0, :, :, -1], h_field[2, :, :, -1])), "col", 1)
        e_field, psi_ele = electric(
            e_field, h_field, psi_ele, e_coef, prev_x, prev_y, edx, egx, edy, egy
        )
    planes = jnp.concatenate((e_field, h_field), 0).reshape(6 * depth_z, rows_here, cols_here)
    snaps = jnp.take(planes, snap_index, axis=0)
    count = snaps.shape[0]
    flat = snaps.reshape(count, rows_here * cols_here)
    gram_part = jnp.dot(flat, flat.T, precision=lax.Precision.HIGHEST) / float(full_x * full_y)
    local_modes = lax.all_to_all(basis, "row", split_axis=1, concat_axis=0, tiled=True)
    coef_part = jnp.dot(
        flat, local_modes.reshape(local_modes.shape[0], -1).T, precision=lax.Precision.HIGHEST
    )
    coefficients, gram = lax.psum((coef_part, gram_part), ("row", "col"))
    return (e_field, h_field, coefficients, gram)


def solution(mesh):
    in_specs = (
        P(None, None, "row", "col"),
        P(None, None, "row", "col"),
        P(None, "row", "col"),
        P("row", None, "col"),
        P(),
        P(),
    )
    out_specs = (P(None, None, "row", "col"), P(None, None, "row", "col"), P(), P())
    return jax.shard_map(shards, mesh=mesh, in_specs=in_specs, out_specs=out_specs, check_vma=False)
```

profile of v0, /device:TPU:0, one launch (start us, length us, event | category | flops | bytes accessed | tf_op | source)
XLA Modules:
  0.0 349.9 jit_solution(4718568576324864153)
XLA Ops:
  6.9 7.1 %all-to-all-start = ((f32[32,32,128]{2,0,1:T(8,128)}), f32[32,32,128]{2,0,1:T(8,128)}, u32[]{:S(2)}, u32[]{:S(2)}) async-start(f32[32,32,128]{2,0,1:T(8,128)} %copy.1592), calls=%async_computation | async-start | bytes 1048576 | tf_op jit(solution)/shard_map/all_to_all | solution.py:118
  30.5 2.8 collective-permute-start.2
  36.1 3.6 %collective-permute-start.3 = (f32[2,64,128]{2,1,0:T(8,128)S(1)}, f32[2,64,128]{2,1,0:T(8,128)S(1)}, u32[]{:S(2)}, u32[]{:S(2)}) collective-permute-start(f32[2,64,128]{2,1,0:T(8,128)S(1)} %bitcast.519), channel_id=1, source_target_pairs={{0,8},{8,16},{16,24},{1,9},{9,17},{17,25},{2,10},{10,18},{18,26},{... | collective-permute-start | bytes 196616 | tf_op jit(solution)/shard_map/ppermute | solution.py:17
  51.8 3.4 collective-permute-done.4
  57.8 2.4 multiply_subtract_fusion.19
  60.4 2.6 collective-permute-start.6
  64.5 5.6 %collective-permute-start.7 = (f32[2,64,128]{2,1,0:T(8,128)}, f32[2,64,128]{2,1,0:T(8,128)}, u32[]{:S(2)}, u32[]{:S(2)}) collective-permute-start(f32[2,64,128]{2,1,0:T(8,128)} %fusion.15), channel_id=1, source_target_pairs={{0,8},{8,16},{16,24},{1,9},{9,17},{17,25},{2,10},{10,18},{18,26},{... | collective-permute-start | bytes 196616 | tf_op jit(solution)/shard_map/ppermute | solution.py:17
  90.2 2.4 multiply_subtract_fusion.17
  93.6 4.2 %collective-permute-start.10 = (f32[2,64,8]{1,2,0:T(8,128)S(1)}, f32[2,64,8]{1,2,0:T(8,128)S(1)}, u32[]{:S(2)}, u32[]{:S(2)}) collective-permute-start(f32[2,64,8]{1,2,0:T(8,128)S(1)} %pad_maximum_fusion.22), channel_id=1, source_target_pairs={{0,1},{1,2},{2,3},{3,4},{4,5},{5,6},{6,7},{8,9},{9,10},{10,11},{11... | collective-permute-start | bytes 12296 | tf_op jit(solution)/shard_map/ppermute | solution.py:17
  101.4 4.9 %collective-permute-start.11 = (f32[2,64,128]{2,1,0:T(8,128)}, f32[2,64,128]{2,1,0:T(8,128)}, u32[]{:S(2)}, u32[]{:S(2)}) collective-permute-start(f32[2,64,128]{2,1,0:T(8,128)} %bitcast.74), channel_id=1, source_target_pairs={{0,8},{8,16},{16,24},{1,9},{9,17},{17,25},{2,10},{10,18},{18,26},{... | collective-permute-start | bytes 196616 | tf_op jit(solution)/shard_map/ppermute | solution.py:17
  124.8 2.3 multiply_subtract_fusion.13
  133.7 4.3 %collective-permute-start.14 = (f32[2,64,8]{1,2,0:T(8,128)S(1)}, f32[2,64,8]{1,2,0:T(8,128)S(1)}, u32[]{:S(2)}, u32[]{:S(2)}) collective-permute-start(f32[2,64,8]{1,2,0:T(8,128)S(1)} %pad_maximum_fusion.24), channel_id=1, source_target_pairs={{0,1},{1,2},{2,3},{3,4},{4,5},{5,6},{6,7},{8,9},{9,10},{10,11},{11... | collective-permute-start | bytes 12296 | tf_op jit(solution)/shard_map/ppermute | solution.py:17
  140.6 4.9 %collective-permute-start.15 = (f32[2,64,128]{2,1,0:T(8,128)}, f32[2,64,128]{2,1,0:T(8,128)}, u32[]{:S(2)}, u32[]{:S(2)}) collective-permute-start(f32[2,64,128]{2,1,0:T(8,128)} %fusion.12), channel_id=1, source_target_pairs={{0,8},{8,16},{16,24},{1,9},{9,17},{17,25},{2,10},{10,18},{18,26},{... | collective-permute-start | bytes 196616 | tf_op jit(solution)/shard_map/ppermute | solution.py:17
  165.2 2.4 multiply_subtract_fusion.11
  167.9 3.1 collective-permute-start.18
  174.5 5.1 %collective-permute-start.19 = (f32[2,64,128]{2,1,0:T(8,128)}, f32[2,64,128]{2,1,0:T(8,128)}, u32[]{:S(2)}, u32[]{:S(2)}) collective-permute-start(f32[2,64,128]{2,1,0:T(8,128)} %bitcast.119), channel_id=1, source_target_pairs={{0,8},{8,16},{16,24},{1,9},{9,17},{17,25},{2,10},{10,18},{18,26},{... | collective-permute-start | bytes 196616 | tf_op jit(solution)/shard_map/ppermute | solution.py:17
  203.1 2.3 multiply_subtract_fusion.8
  207.2 5.1 %collective-permute-start.22 = (f32[2,64,8]{1,2,0:T(8,128)S(1)}, f32[2,64,8]{1,2,0:T(8,128)S(1)}, u32[]{:S(2)}, u32[]{:S(2)}) collective-permute-start(f32[2,64,8]{1,2,0:T(8,128)S(1)} %pad_maximum_fusion.28), channel_id=1, source_target_pairs={{0,1},{1,2},{2,3},{3,4},{4,5},{5,6},{6,7},{8,9},{9,10},{10,11},{11... | collective-permute-start | bytes 12296 | tf_op jit(solution)/shard_map/ppermute | solution.py:17
  215.0 4.9 %collective-permute-start.23 = (f32[2,64,128]{2,1,0:T(8,128)}, f32[2,64,128]{2,1,0:T(8,128)}, u32[]{:S(2)}, u32[]{:S(2)}) collective-permute-start(f32[2,64,128]{2,1,0:T(8,128)} %fusion.9), channel_id=1, source_target_pairs={{0,8},{8,16},{16,24},{1,9},{9,17},{17,25},{2,10},{10,18},{18,26},{... | collective-permute-start | bytes 196616 | tf_op jit(solution)/shard_map/ppermute | solution.py:17
  245.1 3.8 %collective-permute-start.26 = (f32[2,64,8]{1,2,0:T(8,128)S(1)}, f32[2,64,8]{1,2,0:T(8,128)S(1)}, u32[]{:S(2)}, u32[]{:S(2)}) collective-permute-start(f32[2,64,8]{1,2,0:T(8,128)S(1)} %pad_maximum_fusion.30), channel_id=1, source_target_pairs={{0,1},{1,2},{2,3},{3,4},{4,5},{5,6},{6,7},{8,9},{9,10},{10,11},{11... | collective-permute-start | bytes 12296 | tf_op jit(solution)/shard_map/ppermute | solution.py:17
  252.5 4.9 %collective-permute-start.27 = (f32[2,64,128]{2,1,0:T(8,128)}, f32[2,64,128]{2,1,0:T(8,128)}, u32[]{:S(2)}, u32[]{:S(2)}) collective-permute-start(f32[2,64,128]{2,1,0:T(8,128)} %fusion.8), channel_id=1, source_target_pairs={{0,8},{8,16},{16,24},{1,9},{9,17},{17,25},{2,10},{10,18},{18,26},{... | collective-permute-start | bytes 196616 | tf_op jit(solution)/shard_map/ppermute | solution.py:17
  283.2 4.0 %collective-permute-start.30 = (f32[2,64,8]{1,2,0:T(8,128)S(1)}, f32[2,64,8]{1,2,0:T(8,128)S(1)}, u32[]{:S(2)}, u32[]{:S(2)}) collective-permute-start(f32[2,64,8]{1,2,0:T(8,128)S(1)} %pad_maximum_fusion.32), channel_id=1, source_target_pairs={{0,1},{1,2},{2,3},{3,4},{4,5},{5,6},{6,7},{8,9},{9,10},{10,11},{11... | collective-permute-start | bytes 12296 | tf_op jit(solution)/shard_map/ppermute | solution.py:17
  290.3 4.9 %collective-permute-start.31 = (f32[2,64,128]{2,1,0:T(8,128)S(1)}, f32[2,64,128]{2,1,0:T(8,128)}, u32[]{:S(2)}, u32[]{:S(2)}) collective-permute-start(f32[2,64,128]{2,1,0:T(8,128)S(1)} %bitcast.520), channel_id=1, source_target_pairs={{0,8},{8,16},{16,24},{1,9},{9,17},{17,25},{2,10},{10,18},{18,26},{... | collective-permute-start | bytes 196616 | tf_op jit(solution)/shard_map/ppermute | solution.py:17
  307.1 41.9 %all-reduce.32 = (f32[64,128]{1,0:T(8,128)}, f32[64,64]{1,0:T(8,128)}) all-reduce(f32[64,128]{1,0:T(8,128)S(1)} %fusion.1, f32[64,64]{1,0:T(8,128)S(1)} %fusion), channel_id=1, replica_groups=mesh['row'=4,'col'=8] {'row','col'}, use_global_device_ids=true, to_apply=%region_0.1 | all-reduce | flops 12288 | bytes 98304 | tf_op jit(solution)/shard_map/psum | solution.py:122
  (569 shorter events, 213.0 us)
Async XLA Ops:
  1.8 23.4 %collective-permute-start = (f32[2,64,128]{2,1,0:T(8,128)S(1)}, f32[2,64,128]{2,1,0:T(8,128)}, u32[]{:S(2)}, u32[]{:S(2)}) collective-permute-start(f32[2,64,128]{2,1,0:T(8,128)S(1)} %bitcast.521), channel_id=1, source_target_pairs={{8,0},{16,8},{24,16},{9,1},{17,9},{25,17},{10,2},{18,10},{26,18},{... | collective-permute-start | bytes 196616 | tf_op jit(solution)/shard_map/ppermute | solution.py:17
  4.5 19.5 %collective-permute-start.1 = (f32[2,64,8]{1,2,0:T(8,128)S(1)}, f32[2,64,8]{1,2,0:T(8,128)S(1)}, u32[]{:S(2)}, u32[]{:S(2)}) collective-permute-start(f32[2,64,8]{1,2,0:T(8,128)S(1)} %pad_maximum_fusion.17), channel_id=1, source_target_pairs={{1,0},{2,1},{3,2},{4,3},{5,4},{6,5},{7,6},{9,8},{10,9},{11,10},{12... | collective-permute-start | bytes 12296 | tf_op jit(solution)/shard_map/ppermute | solution.py:17
  6.9 114.8 %all-to-all-start = ((f32[32,32,128]{2,0,1:T(8,128)}), f32[32,32,128]{2,0,1:T(8,128)}, u32[]{:S(2)}, u32[]{:S(2)}) async-start(f32[32,32,128]{2,0,1:T(8,128)} %copy.1592), calls=%async_computation | async-start | bytes 1048576 | tf_op jit(solution)/shard_map/all_to_all | solution.py:118
  30.5 9.3 %collective-permute-start.2 = (f32[2,64,8]{1,2,0:T(8,128)S(1)}, f32[2,64,8]{1,2,0:T(8,128)S(1)}, u32[]{:S(2)}, u32[]{:S(2)}) collective-permute-start(f32[2,64,8]{1,2,0:T(8,128)S(1)} %pad_maximum_fusion.18), channel_id=1, source_target_pairs={{0,1},{1,2},{2,3},{3,4},{4,5},{5,6},{6,7},{8,9},{9,10},{10,11},{11... | collective-permute-start | bytes 12296 | tf_op jit(solution)/shard_map/ppermute | solution.py:17
  60.4 9.7 %collective-permute-start.6 = (f32[2,64,8]{1,2,0:T(8,128)S(1)}, f32[2,64,8]{1,2,0:T(8,128)S(1)}, u32[]{:S(2)}, u32[]{:S(2)}) collective-permute-start(f32[2,64,8]{1,2,0:T(8,128)S(1)} %pad_maximum_fusion.20), channel_id=1, source_target_pairs={{0,1},{1,2},{2,3},{3,4},{4,5},{5,6},{6,7},{8,9},{9,10},{10,11},{11... | collective-permute-start | bytes 12296 | tf_op jit(solution)/shard_map/ppermute | solution.py:17
  64.5 9.9 %collective-permute-start.7 = (f32[2,64,128]{2,1,0:T(8,128)}, f32[2,64,128]{2,1,0:T(8,128)}, u32[]{:S(2)}, u32[]{:S(2)}) collective-permute-start(f32[2,64,128]{2,1,0:T(8,128)} %fusion.15), channel_id=1, source_target_pairs={{0,8},{8,16},{16,24},{1,9},{9,17},{17,25},{2,10},{10,18},{18,26},{... | collective-permute-start | bytes 196616 | tf_op jit(solution)/shard_map/ppermute | solution.py:17
  93.6 12.7 %collective-permute-start.10 = (f32[2,64,8]{1,2,0:T(8,128)S(1)}, f32[2,64,8]{1,2,0:T(8,128)S(1)}, u32[]{:S(2)}, u32[]{:S(2)}) collective-permute-start(f32[2,64,8]{1,2,0:T(8,128)S(1)} %pad_maximum_fusion.22), channel_id=1, source_target_pairs={{0,1},{1,2},{2,3},{3,4},{4,5},{5,6},{6,7},{8,9},{9,10},{10,11},{11... | collective-permute-start | bytes 12296 | tf_op jit(solution)/shard_map/ppermute | solution.py:17
  101.4 9.6 %collective-permute-start.11 = (f32[2,64,128]{2,1,0:T(8,128)}, f32[2,64,128]{2,1,0:T(8,128)}, u32[]{:S(2)}, u32[]{:S(2)}) collective-permute-start(f32[2,64,128]{2,1,0:T(8,128)} %bitcast.74), channel_id=1, source_target_pairs={{0,8},{8,16},{16,24},{1,9},{9,17},{17,25},{2,10},{10,18},{18,26},{... | collective-permute-start | bytes 196616 | tf_op jit(solution)/shard_map/ppermute | solution.py:17
  115.3 8.6 %collective-permute-start.13 = (f32[2,64,8]{1,2,0:T(8,128)S(1)}, f32[2,64,8]{1,2,0:T(8,128)S(1)}, u32[]{:S(2)}, u32[]{:S(2)}) collective-permute-start(f32[2,64,8]{1,2,0:T(8,128)S(1)} %pad_maximum_fusion.23), channel_id=1, source_target_pairs={{1,0},{2,1},{3,2},{4,3},{5,4},{6,5},{7,6},{9,8},{10,9},{11,10},{12... | collective-permute-start | bytes 12296 | tf_op jit(solution)/shard_map/ppermute | solution.py:17
  120.3 9.3 %collective-permute-start.12 = (f32[2,64,128]{2,1,0:T(8,128)}, f32[2,64,128]{2,1,0:T(8,128)}, u32[]{:S(2)}, u32[]{:S(2)}) collective-permute-start(f32[2,64,128]{2,1,0:T(8,128)} %fusion.13), channel_id=1, source_target_pairs={{8,0},{16,8},{24,16},{9,1},{17,9},{25,17},{10,2},{18,10},{26,18},{... | collective-permute-start | bytes 196616 | tf_op jit(solution)/shard_map/ppermute | solution.py:17
  133.7 11.8 %collective-permute-start.14 = (f32[2,64,8]{1,2,0:T(8,128)S(1)}, f32[2,64,8]{1,2,0:T(8,128)S(1)}, u32[]{:S(2)}, u32[]{:S(2)}) collective-permute-start(f32[2,64,8]{1,2,0:T(8,128)S(1)} %pad_maximum_fusion.24), channel_id=1, source_target_pairs={{0,1},{1,2},{2,3},{3,4},{4,5},{5,6},{6,7},{8,9},{9,10},{10,11},{11... | collective-permute-start | bytes 12296 | tf_op jit(solution)/shard_map/ppermute | solution.py:17
  140.6 10.4 %collective-permute-start.15 = (f32[2,64,128]{2,1,0:T(8,128)}, f32[2,64,128]{2,1,0:T(8,128)}, u32[]{:S(2)}, u32[]{:S(2)}) collective-permute-start(f32[2,64,128]{2,1,0:T(8,128)} %fusion.12), channel_id=1, source_target_pairs={{0,8},{8,16},{16,24},{1,9},{9,17},{17,25},{2,10},{10,18},{18,26},{... | collective-permute-start | bytes 196616 | tf_op jit(solution)/shard_map/ppermute | solution.py:17
  167.9 11.8 %collective-permute-start.18 = (f32[2,64,8]{1,2,0:T(8,128)S(1)}, f32[2,64,8]{1,2,0:T(8,128)S(1)}, u32[]{:S(2)}, u32[]{:S(2)}) collective-permute-start(f32[2,64,8]{1,2,0:T(8,128)S(1)} %pad_maximum_fusion.26), channel_id=1, source_target_pairs={{0,1},{1,2},{2,3},{3,4},{4,5},{5,6},{6,7},{8,9},{9,10},{10,11},{11... | collective-permute-start | bytes 12296 | tf_op jit(solution)/shard_map/ppermute | solution.py:17
  174.5 9.8 %collective-permute-start.19 = (f32[2,64,128]{2,1,0:T(8,128)}, f32[2,64,128]{2,1,0:T(8,128)}, u32[]{:S(2)}, u32[]{:S(2)}) collective-permute-start(f32[2,64,128]{2,1,0:T(8,128)} %bitcast.119), channel_id=1, source_target_pairs={{0,8},{8,16},{16,24},{1,9},{9,17},{17,25},{2,10},{10,18},{18,26},{... | collective-permute-start | bytes 196616 | tf_op jit(solution)/shard_map/ppermute | solution.py:17
  189.8 7.0 %collective-permute-start.21 = (f32[2,64,8]{1,2,0:T(8,128)S(1)}, f32[2,64,8]{1,2,0:T(8,128)S(1)}, u32[]{:S(2)}, u32[]{:S(2)}) collective-permute-start(f32[2,64,8]{1,2,0:T(8,128)S(1)} %pad_maximum_fusion.27), channel_id=1, source_target_pairs={{1,0},{2,1},{3,2},{4,3},{5,4},{6,5},{7,6},{9,8},{10,9},{11,10},{12... | collective-permute-start | bytes 12296 | tf_op jit(solution)/shard_map/ppermute | solution.py:17
  195.6 6.8 %collective-permute-start.20 = (f32[2,64,128]{2,1,0:T(8,128)}, f32[2,64,128]{2,1,0:T(8,128)}, u32[]{:S(2)}, u32[]{:S(2)}) collective-permute-start(f32[2,64,128]{2,1,0:T(8,128)} %fusion.10), channel_id=1, source_target_pairs={{8,0},{16,8},{24,16},{9,1},{17,9},{25,17},{10,2},{18,10},{26,18},{... | collective-permute-start | bytes 196616 | tf_op jit(solution)/shard_map/ppermute | solution.py:17
  207.2 12.6 %collective-permute-start.22 = (f32[2,64,8]{1,2,0:T(8,128)S(1)}, f32[2,64,8]{1,2,0:T(8,128)S(1)}, u32[]{:S(2)}, u32[]{:S(2)}) collective-permute-start(f32[2,64,8]{1,2,0:T(8,128)S(1)} %pad_maximum_fusion.28), channel_id=1, source_target_pairs={{0,1},{1,2},{2,3},{3,4},{4,5},{5,6},{6,7},{8,9},{9,10},{10,11},{11... | collective-permute-start | bytes 12296 | tf_op jit(solution)/shard_map/ppermute | solution.py:17
  215.0 9.5 %collective-permute-start.23 = (f32[2,64,128]{2,1,0:T(8,128)}, f32[2,64,128]{2,1,0:T(8,128)}, u32[]{:S(2)}, u32[]{:S(2)}) collective-permute-start(f32[2,64,128]{2,1,0:T(8,128)} %fusion.9), channel_id=1, source_target_pairs={{0,8},{8,16},{16,24},{1,9},{9,17},{17,25},{2,10},{10,18},{18,26},{... | collective-permute-start | bytes 196616 | tf_op jit(solution)/shard_map/ppermute | solution.py:17
  227.9 7.4 %collective-permute-start.25 = (f32[2,64,8]{1,2,0:T(8,128)S(1)}, f32[2,64,8]{1,2,0:T(8,128)S(1)}, u32[]{:S(2)}, u32[]{:S(2)}) collective-permute-start(f32[2,64,8]{1,2,0:T(8,128)S(1)} %pad_maximum_fusion.29), channel_id=1, source_target_pairs={{1,0},{2,1},{3,2},{4,3},{5,4},{6,5},{7,6},{9,8},{10,9},{11,10},{12... | collective-permute-start | bytes 12296 | tf_op jit(solution)/shard_map/ppermute | solution.py:17
  245.1 12.3 %collective-permute-start.26 = (f32[2,64,8]{1,2,0:T(8,128)S(1)}, f32[2,64,8]{1,2,0:T(8,128)S(1)}, u32[]{:S(2)}, u32[]{:S(2)}) collective-permute-start(f32[2,64,8]{1,2,0:T(8,128)S(1)} %pad_maximum_fusion.30), channel_id=1, source_target_pairs={{0,1},{1,2},{2,3},{3,4},{4,5},{5,6},{6,7},{8,9},{9,10},{10,11},{11... | collective-permute-start | bytes 12296 | tf_op jit(solution)/shard_map/ppermute | solution.py:17
  252.5 10.2 %collective-permute-start.27 = (f32[2,64,128]{2,1,0:T(8,128)}, f32[2,64,128]{2,1,0:T(8,128)}, u32[]{:S(2)}, u32[]{:S(2)}) collective-permute-start(f32[2,64,128]{2,1,0:T(8,128)} %fusion.8), channel_id=1, source_target_pairs={{0,8},{8,16},{16,24},{1,9},{9,17},{17,25},{2,10},{10,18},{18,26},{... | collective-permute-start | bytes 196616 | tf_op jit(solution)/shard_map/ppermute | solution.py:17
  267.4 7.0 %collective-permute-start.29 = (f32[2,64,8]{1,2,0:T(8,128)S(1)}, f32[2,64,8]{1,2,0:T(8,128)S(1)}, u32[]{:S(2)}, u32[]{:S(2)}) collective-permute-start(f32[2,64,8]{1,2,0:T(8,128)S(1)} %pad_maximum_fusion.31), channel_id=1, source_target_pairs={{1,0},{2,1},{3,2},{4,3},{5,4},{6,5},{7,6},{9,8},{10,9},{11,10},{12... | collective-permute-start | bytes 12296 | tf_op jit(solution)/shard_map/ppermute | solution.py:17
  283.2 11.9 %collective-permute-start.30 = (f32[2,64,8]{1,2,0:T(8,128)S(1)}, f32[2,64,8]{1,2,0:T(8,128)S(1)}, u32[]{:S(2)}, u32[]{:S(2)}) collective-permute-start(f32[2,64,8]{1,2,0:T(8,128)S(1)} %pad_maximum_fusion.32), channel_id=1, source_target_pairs={{0,1},{1,2},{2,3},{3,4},{4,5},{5,6},{6,7},{8,9},{9,10},{10,11},{11... | collective-permute-start | bytes 12296 | tf_op jit(solution)/shard_map/ppermute | solution.py:17
  290.3 7.3 %collective-permute-start.31 = (f32[2,64,128]{2,1,0:T(8,128)S(1)}, f32[2,64,128]{2,1,0:T(8,128)}, u32[]{:S(2)}, u32[]{:S(2)}) collective-permute-start(f32[2,64,128]{2,1,0:T(8,128)S(1)} %bitcast.520), channel_id=1, source_target_pairs={{0,8},{8,16},{16,24},{1,9},{9,17},{17,25},{2,10},{10,18},{18,26},{... | collective-permute-start | bytes 196616 | tf_op jit(solution)/shard_map/ppermute | solution.py:17
  (122 other events, 810.5 us)
where the time goes:
time: 353 us; the launch traced here: 350 us
  local copies, waits for them, and re-layouts  103 us (29%)
  other arithmetic  97 us (27%)
  starting transfers between devices  96.6 us (27%)
  blocking collectives  41.9 us (12%)
  waiting for transfers between devices  6.21 us (2%)
  between operations  4.05 us (1%)
    ppermute x32, starting transfers between devices, from_behind(): return lax.ppermute(block, axis, route)  89.5 us
    psum x1, blocking collectives, shards(): coefficients, gram = lax.psum((coef_part, gram_part), ('row', 'col'))  41.9 us
    slice x45, local copies, waits for them, and re-layouts, forward(): lax.slice_in_dim(field, 1, count, axis=axis)  33.3 us
    sub x8, other arithmetic, magnetic(): h_z = h_z - time_step * (ey_dx + psi_hzx - ex_dy - psi_hzy)  15.1 us
    sub x8, other arithmetic, magnetic(): h_x = h_x - time_step * (ez_dy + psi_hxy - ey_dz)  14.6 us
    another operation x24, local copies, waits for them, and re-layouts, forward(): jnp.expand_dims(plane, axis)  12.5 us
    sub x7, other arithmetic, magnetic(): h_y = h_y - time_step * (ex_dz - ez_dx - psi_hyx)  12 us
    add x6, other arithmetic, electric(): e_z = e_z + e_coef * (hy_dx + psi_ezx - hx_dy - psi_ezy)  10.3 us
  transfers between devices with their start and end apart: 33, of which 5 were waited for; matrix products, arithmetic and copies ran while one was open for 43% of the time, Pallas kernels for 0%

commit v1 on v0

v1 whole, which is shorter than its diff:
```python
import functools
import jax
import jax.numpy as jnp
from jax import lax
from jax.experimental import pallas as pl
from jax.experimental.pallas import tpu as pltpu
from jax.sharding import PartitionSpec as P

STEPS = 8
UNROLL = 4

time_step = 0.5
sigma_top = 4.0
alpha_shift = 0.05


def absorber(positions, total, low, high):
    depth = jnp.maximum(
        jnp.maximum((low - positions) / low, (positions - (total - 1.0 - high)) / high), 0.0
    )
    sigma = sigma_top * (depth * depth * depth)
    damp = jnp.exp(-(sigma + alpha_shift) * time_step)
    gain = sigma / (sigma + alpha_shift) * (damp - 1.0)
    return damp, gain


def step_kernel(
    n_row, n_col, width_ref, e_in, h_in, coef_in, e_out, h_out,
    e_s, h_s, coef_s, psi, first_x, last_x, h_last_x, first_y, last_y, h_last_y,
    next_x, prev_x, halo_x, halo_psi_x, next_y, prev_y, corner_x, corner_y, halo_y, halo_psi_y,
    prof, local_sem, send_sem, recv_sem, once_send, once_recv,
):
    nz, nx, ny = coef_s.shape
    row, col = lax.axis_index("row"), lax.axis_index("col")
    up, down = row > 0, row < n_row - 1
    left, right = col > 0, col < n_col - 1
    sw = jnp.logical_and(down, left)
    ne = jnp.logical_and(up, right)
    routes = (
        (up, {"row": row - 1, "col": col}), (down, {"row": row + 1, "col": col}),
        (left, {"row": row, "col": col - 1}), (sw, {"row": row + 1, "col": col - 1}),
        (right, {"row": row, "col": col + 1}), (ne, {"row": row - 1, "col": col + 1}),
    )

    load_e = pltpu.make_async_copy(e_in, e_s.at[:, pl.ds(0, nz)], local_sem.at[0])
    load_h = pltpu.make_async_copy(h_in, h_s.at[:, pl.ds(1, nz)], local_sem.at[1])
    load_c = pltpu.make_async_copy(coef_in, coef_s, local_sem.at[2])
    load_e.start()
    load_h.start()
    load_c.start()

    next_x[...] = jnp.zeros_like(next_x)
    prev_x[...] = jnp.zeros_like(prev_x)
    halo_x[...] = jnp.zeros_like(halo_x)
    halo_psi_x[...] = jnp.zeros_like(halo_psi_x)
    next_y[...] = jnp.zeros_like(next_y)
    prev_y[...] = jnp.zeros_like(prev_y)
    corner_x[...] = jnp.zeros_like(corner_x)
    corner_y[...] = jnp.zeros_like(corner_y)
    halo_y[...] = jnp.zeros_like(halo_y)
    halo_psi_y[...] = jnp.zeros_like(halo_psi_y)

    barrier = pltpu.get_barrier_semaphore()
    for there, where in routes:
        @pl.when(there)
        def _():
            pl.semaphore_signal(barrier, inc=1, device_id=where, device_id_type=pl.DeviceIdType.MESH)

    zero = jnp.zeros((nx, ny), jnp.float32)
    for c in range(3):
        e_s[c, nz] = zero
        h_s[c, 0] = zero

    def clear(z, carry):
        for k in range(8):
            psi[k, z] = zero
        return carry

    lax.fori_loop(0, nz, clear, 0)

    sub = lax.broadcasted_iota(jnp.int32, (nx, ny), 0)
    lane = lax.broadcasted_iota(jnp.int32, (nx, ny), 1)
    w = [jnp.full((nx, ny), width_ref[k], jnp.int32).astype(jnp.float32) for k in range(4)]
    x_pos = (sub + row * nx).astype(jnp.float32)
    y_pos = (lane + col * ny).astype(jnp.float32)
    x_before = (jnp.zeros_like(sub) + (row * nx - 1)).astype(jnp.float32)
    y_before = (jnp.zeros_like(sub) + (col * ny - 1)).astype(jnp.float32)
    full_x, full_y = float(nx * n_row), float(ny * n_col)
    pairs = (
        absorber(x_pos + 0.5, full_x, w[0], w[1]), absorber(y_pos + 0.5, full_y, w[2], w[3]),
        absorber(x_pos, full_x, w[0], w[1]), absorber(y_pos, full_y, w[2], w[3]),
        absorber(x_before + 0.5, full_x, w[0], w[1]), absorber(y_before + 0.5, full_y, w[2], w[3]),
    )
    for k, (damp, gain) in enumerate(pairs):
        prof[2 * k] = damp
        prof[2 * k + 1] = gain

    def pack(z, ex, ey, ez, cols):
        first, last0, last1 = cols
        first_x[0, pl.ds(z, 1), :] = ey[0:1]
        first_x[1, pl.ds(z, 1), :] = ez[0:1]
        last_x[0, pl.ds(z, 1), :] = ex[nx - 1:nx]
        last_x[1, pl.ds(z, 1), :] = ey[nx - 1:nx]
        last_x[2, pl.ds(z, 1), :] = ez[nx - 1:nx]
        rx = pltpu.roll(ex, z, 1)
        rz = pltpu.roll(ez, z + nz, 1)
        ry = pltpu.roll(ey, z, 1)
        first = jnp.where(lane == z, rx, jnp.where(lane == z + nz, rz, first))
        before = lax.rem(z + ny - 1, ny)
        last0 = jnp.where(lane == before, rx, jnp.where(lane == z + nz - 1, rz, last0))
        last1 = jnp.where(lane == before, ry, last1)
        return first, last0, last1

    def keep(cols):
        first_y[...] = cols[0]
        last_y[0] = pltpu.roll(cols[1], 1, 1)
        last_y[1] = pltpu.roll(cols[2], 1, 1)

    def copies(slot):
        parts = (
            (first_x, next_x.at[slot]),
            (last_x, prev_x.at[slot, :, pl.ds(0, nz)]),
            (first_y, next_y.at[slot]),
            (first_y, corner_x.at[slot]),
            (last_y, prev_y.at[slot]),
            (last_y.at[1], corner_y.at[slot]),
        )
        return [
            pltpu.make_async_remote_copy(
                src_ref=src, dst_ref=dst, send_sem=send_sem.at[m, slot], recv_sem=recv_sem.at[m, slot],
                device_id=routes[m][1], device_id_type=pl.DeviceIdType.MESH)
            for m, (src, dst) in enumerate(parts)
        ]

    def start_all(slot):
        for m, copy in enumerate(copies(slot)):
            @pl.when(routes[m][0])
            def _():
                copy.start()

    arrives = (down, up, right, ne, left, sw)

    def wait_recv(slot, which):
        every = copies(slot)
        for m in which:
            @pl.when(arrives[m])
            def _():
                every[m].wait_recv()

    def wait_send(slot):
        for m, copy in enumerate(copies(slot)):
            @pl.when(routes[m][0])
            def _():
                copy.wait_send()

    load_e.wait()
    load_h.wait()

    def first_pack(k, carry):
        cols, hcol = carry
        for j in range(UNROLL):
            z = k * UNROLL + j
            cols = pack(z, e_s[0, z], e_s[1, z], e_s[2, z], cols)
            hx, hy, hz = h_s[0, z + 1], h_s[1, z + 1], h_s[2, z + 1]
            h_last_x[0, pl.ds(z, 1), :] = hy[nx - 1:nx]
            h_last_x[1, pl.ds(z, 1), :] = hz[nx - 1:nx]
            hcol = jnp.where(lane == z, pltpu.roll(hz, z + 1, 1), hcol)
            hcol = jnp.where(lane == z + nz, pltpu.roll(hx, lax.rem(z + nz + 1, ny), 1), hcol)
        return cols, hcol

    cols, hcol = lax.fori_loop(0, nz // UNROLL, first_pack, ((zero, zero, zero), zero))
    keep(cols)
    h_last_y[...] = hcol

    count = sum(there.astype(jnp.int32) for there, _ in routes)
    pl.semaphore_wait(barrier, count)
    once = [
        pltpu.make_async_remote_copy(
            src_ref=src, dst_ref=dst, send_sem=once_send.at[k], recv_sem=once_recv.at[k],
            device_id=routes[m][1], device_id_type=pl.DeviceIdType.MESH)
        for k, (src, dst, m) in enumerate(((h_last_x, halo_x, 1), (h_last_y, halo_y, 4)))
    ]
    start_all(0)
    for k, m in enumerate((1, 4)):
        @pl.when(routes[m][0])
        def _():
            once[k].start()
    load_c.wait()

    def magnetic(slot):
        hdx, hgx, hdy, hgy = prof[0], prof[1], prof[2], prof[3]
        edge = next_y[slot]

        def body(k, carry):
            for j in range(UNROLL):
                z = k * UNROLL + j
                ex, ey, ez = e_s[0, z], e_s[1, z], e_s[2, z]
                row_y = jnp.broadcast_to(next_x[slot, 0, pl.ds(z, 1), :], (nx, ny))
                row_z = jnp.broadcast_to(next_x[slot, 1, pl.ds(z, 1), :], (nx, ny))
                col_x = pltpu.roll(edge, ny - 1 - z, 1)
                col_z = pltpu.roll(edge, ny - 1 - nz - z, 1)
                ey_dz = e_s[1, z + 1] - ey
                ex_dz = e_s[0, z + 1] - ex
                ez_dy = jnp.where(lane == ny - 1, col_z, pltpu.roll(ez, ny - 1, 1)) - ez
                ex_dy = jnp.where(lane == ny - 1, col_x, pltpu.roll(ex, ny - 1, 1)) - ex
                ez_dx = jnp.where(sub == nx - 1, row_z, pltpu.roll(ez, nx - 1, 0)) - ez
                ey_dx = jnp.where(sub == nx - 1, row_y, pltpu.roll(ey, nx - 1, 0)) - ey
                p0 = hdy * psi[0, z] + hgy * ez_dy
                p1 = hdx * psi[1, z] + hgx * ez_dx
                p2 = hdx * psi[2, z] + hgx * ey_dx
                p3 = hdy * psi[3, z] + hgy * ex_dy
                psi[0, z], psi[1, z], psi[2, z], psi[3, z] = p0, p1, p2, p3
                h_s[0, z + 1] = h_s[0, z + 1] - time_step * (ez_dy + p0 - ey_dz)
                h_s[1, z + 1] = h_s[1, z + 1] - time_step * (ex_dz - ez_dx - p1)
                h_s[2, z + 1] = h_s[2, z + 1] - time_step * (ey_dx + p2 - ex_dy - p3)
            return carry

        lax.fori_loop(0, nz // UNROLL, body, 0)

    def magnetic_row_before(slot):
        hdy, hgy = prof[2][0:1], prof[3][0:1]
        hdx, hgx = prof[8][0:1], prof[9][0:1]
        ex, ey, ez = prev_x[slot, 0, 0:nz], prev_x[slot, 1, 0:nz], prev_x[slot, 2, 0:nz]
        big_lane = lax.broadcasted_iota(jnp.int32, (nz, ny), 1)
        big_z = lax.broadcasted_iota(jnp.int32, (nz, ny), 0)
        corner = jnp.broadcast_to(corner_x[slot, nx - 1:nx, :], (nz, ny))
        corner = jnp.sum(jnp.where(big_lane == big_z, corner, 0.0), axis=1, keepdims=True)
        ex_dz = prev_x[slot, 0, 1:nz + 1] - ex
        ex_dy = jnp.where(big_lane == ny - 1, corner, pltpu.roll(ex, ny - 1, 1)) - ex
        ey_dx = first_x[0] - ey
        ez_dx = first_x[1] - ez
        p1 = hdx * halo_psi_x[0] + hgx * ez_dx
        p2 = hdx * halo_psi_x[1] + hgx * ey_dx
        p3 = hdy * halo_psi_x[2] + hgy * ex_dy
        halo_psi_x[0], halo_psi_x[1], halo_psi_x[2] = p1, p2, p3
        mask = up.astype(jnp.float32)
        halo_x[0] = mask * (halo_x[0] - time_step * (ex_dz - ez_dx - p1))
        halo_x[1] = mask * (halo_x[1] - time_step * (ey_dx + p2 - ex_dy - p3))

    def magnetic_column_before(slot):
        hdx, hgx = prof[0], prof[1]
        hdy, hgy = prof[10], prof[11]
        ey = prev_y[slot, 1]
        dy = first_y[...] - prev_y[slot, 0]
        below = jnp.broadcast_to(corner_y[slot, 0:1, :], (nx, ny))
        ey_dx = jnp.where(sub == nx - 1, below, pltpu.roll(ey, nx - 1, 0)) - ey
        ey_dz = pltpu.roll(pltpu.roll(ey, ny - 1, 1) - ey, nz, 1)
        py = hdy * halo_psi_y[0] + hgy * dy
        px = hdx * halo_psi_y[1] + hgx * ey_dx
        halo_psi_y[0], halo_psi_y[1] = py, px
        mask = left.astype(jnp.float32)
        change = jnp.where(lane < nz, ey_dx + px - dy - py, dy + py - ey_dz)
        halo_y[...] = mask * (halo_y[...] - time_step * change)

    def electric():
        edx, egx, edy, egy = prof[4], prof[5], prof[6], prof[7]
        edge = halo_y[...]

        def body(k, cols):
            for j in range(UNROLL):
                z = k * UNROLL + j
                hx, hy, hz = h_s[0, z + 1], h_s[1, z + 1], h_s[2, z + 1]
                row_y = jnp.broadcast_to(halo_x[0, pl.ds(z, 1), :], (nx, ny))
                row_z = jnp.broadcast_to(halo_x[1, pl.ds(z, 1), :], (nx, ny))
                col_z = pltpu.roll(edge, lax.rem(ny - z, ny), 1)
                col_x = pltpu.roll(edge, ny - nz - z, 1)
                hy_dz = hy - h_s[1, z]
                hx_dz = hx - h_s[0, z]
                hz_dy = hz - jnp.where(lane == 0, col_z, pltpu.roll(hz, 1, 1))
                hx_dy = hx - jnp.where(lane == 0, col_x, pltpu.roll(hx, 1, 1))
                hz_dx = hz - jnp.where(sub == 0, row_z, pltpu.roll(hz, 1, 0))
                hy_dx = hy - jnp.where(sub == 0, row_y, pltpu.roll(hy, 1, 0))
                p0 = edy * psi[4, z] + egy * hz_dy
                p1 = edx * psi[5, z] + egx * hz_dx
                p2 = edx * psi[6, z] + egx * hy_dx
                p3 = edy * psi[7, z] + egy * hx_dy
                psi[4, z], psi[5, z], psi[6, z], psi[7, z] = p0, p1, p2, p3
                amount = coef_s[z]
                ex = e_s[0, z] + amount * (hz_dy + p0 - hy_dz)
                ey = e_s[1, z] + amount * (hx_dz - hz_dx - p1)
                ez = e_s[2, z] + amount * (hy_dx + p2 - hx_dy - p3)
                e_s[0, z], e_s[1, z], e_s[2, z] = ex, ey, ez
                cols = pack(z, ex, ey, ez, cols)
            return cols

        keep(lax.fori_loop(0, nz // UNROLL, body, (zero, zero, zero)))

    def step(s, carry):
        slot = lax.rem(s, 2)
        wait_recv(slot, (0, 2))
        magnetic(slot)
        wait_recv(slot, (1, 3))

        @pl.when(s == 0)
        def _():
            for k, there in enumerate((up, left)):
                @pl.when(there)
                def _():
                    once[k].wait_recv()

        magnetic_row_before(slot)
        wait_recv(slot, (4, 5))
        magnetic_column_before(slot)
        wait_send(slot)
        electric()

        @pl.when(s < STEPS - 1)
        def _():
            start_all(1 - slot)

        return carry

    lax.fori_loop(0, STEPS, step, 0)
    for k, m in enumerate((1, 4)):
        @pl.when(routes[m][0])
        def _():
            once[k].wait_send()
    store_e = pltpu.make_async_copy(e_s.at[:, pl.ds(0, nz)], e_out, local_sem.at[0])
    store_h = pltpu.make_async_copy(h_s.at[:, pl.ds(1, nz)], h_out, local_sem.at[1])
    store_e.start()
    store_h.start()
    store_e.wait()
    store_h.wait()


def run_steps(e_field, h_field, e_coef, pml_width):
    nz, nx, ny = e_coef.shape
    n_row, n_col = lax.axis_size("row"), lax.axis_size("col")
    f32 = jnp.float32
    any_space = pl.BlockSpec(memory_space=pl.ANY)
    return pl.pallas_call(
        functools.partial(step_kernel, n_row, n_col),
        out_shape=[jax.ShapeDtypeStruct(e_field.shape, f32)] * 2,
        in_specs=[pl.BlockSpec(memory_space=pltpu.SMEM), any_space, any_space, any_space],
        out_specs=[any_space, any_space],
        scratch_shapes=[
            pltpu.VMEM((3, nz + 1, nx, ny), f32), pltpu.VMEM((3, nz + 1, nx, ny), f32),
            pltpu.VMEM((nz, nx, ny), f32), pltpu.VMEM((8, nz, nx, ny), f32),
            pltpu.VMEM((2, nz, ny), f32), pltpu.VMEM((3, nz, ny), f32), pltpu.VMEM((2, nz, ny), f32),
            pltpu.VMEM((nx, ny), f32), pltpu.VMEM((2, nx, ny), f32), pltpu.VMEM((nx, ny), f32),
            pltpu.VMEM((2, 2, nz, ny), f32), pltpu.VMEM((2, 3, nz + 8, ny), f32),
            pltpu.VMEM((2, nz, ny), f32), pltpu.VMEM((3, nz, ny), f32),
            pltpu.VMEM((2, nx, ny), f32), pltpu.VMEM((2, 2, nx, ny), f32),
            pltpu.VMEM((2, nx, ny), f32), pltpu.VMEM((2, nx, ny), f32),
            pltpu.VMEM((nx, ny), f32), pltpu.VMEM((2, nx, ny), f32),
            pltpu.VMEM((12, nx, ny), f32),
            pltpu.SemaphoreType.DMA((3,)),
            pltpu.SemaphoreType.DMA((6, 2)), pltpu.SemaphoreType.DMA((6, 2)),
            pltpu.SemaphoreType.DMA((2,)), pltpu.SemaphoreType.DMA((2,)),
        ],
        compiler_params=pltpu.CompilerParams(
            collective_id=0, has_side_effects=True, vmem_limit_bytes=32 * 1024 * 1024
        ),
    )(pml_width, e_field, h_field, e_coef)


def shards(e_field, h_field, e_coef, basis, pml_width, snap_index):
    depth_z, rows_here, cols_here = e_coef.shape
    full_x = rows_here * lax.axis_size("row")
    full_y = cols_here * lax.axis_size("col")
    e_field, h_field = run_steps(e_field, h_field, e_coef, pml_width)
    planes = jnp.concatenate((e_field, h_field), 0).reshape(6 * depth_z, rows_here, cols_here)
    snaps = jnp.take(planes, snap_index, axis=0)
    count = snaps.shape[0]
    flat = snaps.reshape(count, rows_here * cols_here)
    gram_part = jnp.dot(flat, flat.T, precision=lax.Precision.HIGHEST) / float(full_x * full_y)
    local_modes = lax.all_to_all(basis, "row", split_axis=1, concat_axis=0, tiled=True)
    coef_part = jnp.dot(
        flat, local_modes.reshape(local_modes.shape[0], -1).T, precision=lax.Precision.HIGHEST
    )
    coefficients, gram = lax.psum((coef_part, gram_part), ("row", "col"))
    return (e_field, h_field, coefficients, gram)


def solution(mesh):
    in_specs = (
        P(None, None, "row", "col"),
        P(None, None, "row", "col"),
        P(None, "row", "col"),
        P("row", None, "col"),
        P(),
        P(),
    )
    out_specs = (P(None, None, "row", "col"), P(None, None, "row", "col"), P(), P())
    return jax.shard_map(shards, mesh=mesh, in_specs=in_specs, out_specs=out_specs, check_vma=False)
```

time: 353 us -> 131 us (0.37)
  local copies, waits for them, and re-layouts: 103 us -> 6.03 us
  other arithmetic: 97 us -> 0.25 us
  starting transfers between devices: 96.6 us -> 5.19 us
  Pallas kernels: 0 us -> 77.1 us
  waiting for transfers between devices: 6.21 us -> 0.01 us
    ppermute x32 -> x0, starting transfers between devices: 89.5 us -> none  [from_behind(): return lax.ppermute(block, axis, route)]
    pallas_call x0 -> x1, Pallas kernels: none -> 77.1 us  [run_steps(): pl.pallas_call(functools.partial(step_kernel, n_row, n_col), out_shape=[j...]
    slice x123 -> x0, local copies, waits for them, and re-layouts: 70.3 us -> none  [the longest x45 33.3 us: forward(): lax.slice_in_dim(field, 1, count, axis=axis)]
    sub x23 -> x0, other arithmetic: 41.7 us -> none  [the longest x8 15.1 us: magnetic(): h_z = h_z - time_step * (ey_dx + psi_hzx - ex_dy - psi_hzy)]
    add x20 -> x0, other arithmetic: 25.5 us -> none  [the longest x6 10.3 us: electric(): e_z = e_z + e_coef * (hy_dx + psi_ezx - hx_dy - psi_ezy)]
    another operation x68 -> x0, local copies, waits for them, and re-layouts: 23.2 us -> none  [the longest x24 12.5 us: forward(): jnp.expand_dims(plane, axis)]
    another operation x23 -> x0, other arithmetic: 10.5 us -> none  [the longest x8 3.61 us: shards(): jnp.stack((h_field[0, :, :, -1], h_field[2, :, :, -1]))]
    squeeze x10 -> x0, other arithmetic: 7.16 us -> none  [the longest x6 4.64 us: shards(): next_x = from_behind(e_field[1:3, :, 0, :], 'row', -1)]
  transfers between devices with their start and end apart: 33 -> 1, of which waited for: 5 -> 0; matrix products, arithmetic and copies ran while one was open for 43% -> 1% of each run, Pallas kernels for 0% -> 59%
where the time goes in v1:
time: 131 us; the launch traced here: 130 us
  Pallas kernels  77.1 us (59%)
  blocking collectives  39.9 us (30%)
  local copies, waits for them, and re-layouts  6.03 us (5%)
  starting transfers between devices  5.19 us (4%)
    pallas_call x1, Pallas kernels, run_steps(): pl.pallas_call(functools.partial(step_kernel, n_row, n_col), out_shape=[j...  77.1 us
    psum x1, blocking collectives, shards(): coefficients, gram = lax.psum((coef_part, gram_part), ('row', 'col'))  39.9 us
    all_to_all x1, starting transfers between devices, shards(): lax.all_to_all(basis, 'row', split_axis=1, concat_axis=0, tiled=True)  5.19 us
    unnamed x13, local copies, waits for them, and re-layouts  4.05 us
  transfers between devices with their start and end apart: 1, of which 0 were waited for; matrix products, arithmetic and copies ran while one was open for 1% of the time, Pallas kernels for 59%

profile of v1, /device:TPU:0, one launch (start us, length us, event | category | flops | bytes accessed | tf_op | source)
XLA Modules:
  0.0 130.2 jit_solution(3644220539183319144)
XLA Ops:
  0.6 0.0 copy-start.4
  0.6 0.0 copy-start.3
  0.7 0.0 copy-start
  0.7 0.0 copy-start.1
  0.7 0.0 copy-start.2
  0.7 2.3 %copy.13 = f32[32,32,128]{2,0,1:T(8,128)} copy(f32[32,32,128]{2,1,0:T(8,128)} %param.9) | data formatting | bytes 1048576 | tf_op args[3]
  3.0 5.2 %all-to-all-start = ((f32[32,32,128]{2,0,1:T(8,128)}), f32[32,32,128]{2,0,1:T(8,128)}, u32[]{:S(2)}, u32[]{:S(2)}) async-start(f32[32,32,128]{2,0,1:T(8,128)} %copy.13), calls=%async_computation | async-start | bytes 1048576 | tf_op jit(solution)/shard_map/all_to_all | solution.py:367
  8.1 0.0 copy-done.4
  8.2 0.0 copy-done.3
  8.2 0.0 copy-done
  8.2 0.0 copy-done.1
  8.2 0.0 copy-done.2
  8.2 77.1 %shard_map.93 = (f32[3,64,8,128]{3,2,1,0:T(8,128)S(1)}, f32[3,64,8,128]{3,2,1,0:T(8,128)S(1)}) custom-call(s32[4]{0:T(128)S(1)} %copy-done.3, f32[3,64,8,128]{3,2,1,0:T(8,128)S(1)} %copy-done, f32[3,64,8,128]{3,2,1,0:T(8,128)S(1)} %copy-done.1, f32[64,8,128]{2,1,0:T(8,128)S(1)} %copy-done.2), custom_call_target="tpu_custom_call" | custom-call | tf_op jit(solution)/shard_map/pallas_call | solution.py:331
  85.3 0.1 pad_maximum_fusion
  85.4 0.6 gather_fusion
  86.0 0.1 broadcast_select_fusion
  86.2 0.4 fusion
  86.5 0.0 all-to-all-done
  86.6 1.3 %copy.14 = f32[32,4,8,128]{3,2,0,1:T(8,128)S(1)} copy(f32[32,4,8,128]{3,0,2,1:T(8,128)} %bitcast.1) | data formatting | bytes 1048576 | tf_op jit(solution)/shard_map/all_to_all | solution.py:367
  87.9 0.7 fusion.1
  88.6 39.9 %all-reduce = (f32[64,128]{1,0:T(8,128)}, f32[64,64]{1,0:T(8,128)}) all-reduce(f32[64,128]{1,0:T(8,128)S(1)} %fusion.1, f32[64,64]{1,0:T(8,128)S(1)} %fusion), channel_id=1, replica_groups=mesh['row'=4,'col'=8] {'row','col'}, use_global_device_ids=true, to_apply=%region_0.1 | all-reduce | flops 12288 | bytes 98304 | tf_op jit(solution)/shard_map/psum | solution.py:371
  128.4 0.9 copy.31
  129.3 0.9 copy.32
  (3 shorter events, 0.0 us)
Async XLA Ops:
  0.6 7.5 %copy-start.4 = (s32[64]{0:T(128)S(1)}, s32[64]{0:T(128)}, u32[]{:S(2)}) copy-start(s32[64]{0:T(128)} %param.11) | copy-start | bytes 772
  0.6 7.5 %copy-start.3 = (s32[4]{0:T(128)S(1)}, s32[4]{0:T(128)}, u32[]{:S(2)}) copy-start(s32[4]{0:T(128)} %width_ref.1) | copy-start | bytes 52
  0.7 7.5 %copy-start = (f32[3,64,8,128]{3,2,1,0:T(8,128)S(1)}, f32[3,64,8,128]{3,2,1,0:T(8,128)}, u32[]{:S(2)}) copy-start(f32[3,64,8,128]{3,2,1,0:T(8,128)} %e_in.1) | copy-start | bytes 2359300
  0.7 7.5 %copy-start.1 = (f32[3,64,8,128]{3,2,1,0:T(8,128)S(1)}, f32[3,64,8,128]{3,2,1,0:T(8,128)}, u32[]{:S(2)}) copy-start(f32[3,64,8,128]{3,2,1,0:T(8,128)} %h_in.1) | copy-start | bytes 2359300
  0.7 7.5 %copy-start.2 = (f32[64,8,128]{2,1,0:T(8,128)S(1)}, f32[64,8,128]{2,1,0:T(8,128)}, u32[]{:S(2)}) copy-start(f32[64,8,128]{2,1,0:T(8,128)} %coef_in.1) | copy-start | bytes 786436
  3.0 83.6 %all-to-all-start = ((f32[32,32,128]{2,0,1:T(8,128)}), f32[32,32,128]{2,0,1:T(8,128)}, u32[]{:S(2)}, u32[]{:S(2)}) async-start(f32[32,32,128]{2,0,1:T(8,128)} %copy.13), calls=%async_computation | async-start | bytes 1048576 | tf_op jit(solution)/shard_map/all_to_all | solution.py:367

commit v2 on v1

--- a/solution.py
+++ b/solution.py
@@ -7,7 +7,7 @@
 from jax.sharding import PartitionSpec as P
 
 STEPS = 8
-UNROLL = 4
+UNROLL = 16
 
 time_step = 0.5
 sigma_top = 4.0
@@ -25,11 +25,14 @@
 
 
 def step_kernel(
-    n_row, n_col, width_ref, e_in, h_in, coef_in, e_out, h_out,
-    e_s, h_s, coef_s, psi, first_x, last_x, h_last_x, first_y, last_y, h_last_y,
+    n_row, n_col, width_ref, index_ref, e_in, h_in, coef_in, basis_in, e_out, h_out, proj_out, gram_out,
+    fields, coef_s, psi, first_x, last_x, h_last_x, first_y, last_y, h_last_y,
     next_x, prev_x, halo_x, halo_psi_x, next_y, prev_y, corner_x, corner_y, halo_y, halo_psi_y,
-    prof, local_sem, send_sem, recv_sem, once_send, once_recv,
+    prof, modes, snaps, part, row_sums, col_sums, total,
+    local_sem, send_sem, recv_sem, once_send, once_recv, mode_send, mode_recv,
+    sum_send, sum_recv, col_send, col_recv, back_send, back_recv,
 ):
+    e_s, h_s = fields.at[pl.ds(0, 3)], fields.at[pl.ds(3, 3)]
     nz, nx, ny = coef_s.shape
     row, col = lax.axis_index("row"), lax.axis_index("col")
     up, down = row > 0, row < n_row - 1
@@ -48,7 +51,16 @@
     load_e.start()
     load_h.start()
     load_c.start()
-
+    n_modes = basis_in.shape[0]
+    modes_3d = modes.reshape(n_modes * n_row, nx, ny)
+    load_b = pltpu.make_async_copy(
+        basis_in.at[:, pl.ds(pl.multiple_of(row * nx, nx), nx)],
+        modes_3d.at[pl.ds(row * n_modes, n_modes)], local_sem.at[3])
+    load_b.start()
+    row_peers = [lax.rem(row + k, n_row) for k in range(1, n_row)]
+    col_peers = [lax.rem(col + k, n_col) for k in range(1, n_col)]
+
+    part[...] = jnp.zeros_like(part)
     next_x[...] = jnp.zeros_like(next_x)
     prev_x[...] = jnp.zeros_like(prev_x)
     halo_x[...] = jnp.zeros_like(halo_x)
@@ -61,10 +73,17 @@
     halo_psi_y[...] = jnp.zeros_like(halo_psi_y)
 
     barrier = pltpu.get_barrier_semaphore()
-    for there, where in routes:
-        @pl.when(there)
+    for peer in row_peers:
+        pl.semaphore_signal(
+            barrier, inc=1, device_id={"row": peer, "col": col}, device_id_type=pl.DeviceIdType.MESH)
+    for peer in col_peers:
+        pl.semaphore_signal(
+            barrier, inc=1, device_id={"row": row, "col": peer}, device_id_type=pl.DeviceIdType.MESH)
+    for m in (3, 5):
+        @pl.when(routes[m][0])
         def _():
-            pl.semaphore_signal(barrier, inc=1, device_id=where, device_id_type=pl.DeviceIdType.MESH)
+            pl.semaphore_signal(
+                barrier, inc=1, device_id=routes[m][1], device_id_type=pl.DeviceIdType.MESH)
 
     zero = jnp.zeros((nx, ny), jnp.float32)
     for c in range(3):
@@ -172,7 +191,7 @@
     keep(cols)
     h_last_y[...] = hcol
 
-    count = sum(there.astype(jnp.int32) for there, _ in routes)
+    count = n_row - 1 + n_col - 1 + sw.astype(jnp.int32) + ne.astype(jnp.int32)
     pl.semaphore_wait(barrier, count)
     once = [
         pltpu.make_async_remote_copy(
@@ -186,6 +205,17 @@
         def _():
             once[k].start()
     load_c.wait()
+    piece = n_modes // STEPS
+
+    def mode_copies(s):
+        return [
+            pltpu.make_async_remote_copy(
+                src_ref=basis_in.at[pl.ds(s * piece, piece), pl.ds(pl.multiple_of(peer * nx, nx), nx)],
+                dst_ref=modes_3d.at[pl.ds(row * n_modes + s * piece, piece)],
+                send_sem=mode_send.at[k, s], recv_sem=mode_recv.at[k, s],
+                device_id={"row": peer, "col": col}, device_id_type=pl.DeviceIdType.MESH)
+            for k, peer in enumerate(row_peers)
+        ]
 
     def magnetic(slot):
         hdx, hgx, hdy, hgy = prof[0], prof[1], prof[2], prof[3]
@@ -287,6 +317,8 @@
 
     def step(s, carry):
         slot = lax.rem(s, 2)
+        for copy in mode_copies(s):
+            copy.start()
         wait_recv(slot, (0, 2))
         magnetic(slot)
         wait_recv(slot, (1, 3))
@@ -319,22 +351,91 @@
     store_h = pltpu.make_async_copy(h_s.at[:, pl.ds(1, nz)], h_out, local_sem.at[1])
     store_e.start()
     store_h.start()
+
+    count = snaps.shape[0] // nx
+
+    def pick(s, carry):
+        index = index_ref[s]
+        c = index // nz
+        z = index - c * nz + (c // 3)
+        snaps[pl.ds(pl.multiple_of(s * nx, nx), nx), :] = fields[c, z]
+        return carry
+
+    lax.fori_loop(0, count, pick, 0)
+    load_b.wait()
+
+    def wait_modes(s, carry):
+        for copy in mode_copies(s):
+            copy.wait()
+        return carry
+
+    lax.fori_loop(0, STEPS, wait_modes, 0)
+    n_all = modes.shape[0] // nx
+    dims = (((1,), (1,)), ((), ()))
+    proj, gram = None, None
+    for x in range(nx):
+        a = snaps[pl.ds(x, count, stride=nx), :]
+        b = modes[pl.ds(x, n_all, stride=nx), :]
+        p = lax.dot_general(a, b, dims, precision=lax.Precision.HIGHEST, preferred_element_type=jnp.float32)
+        g = lax.dot_general(a, a, dims, precision=lax.Precision.HIGHEST, preferred_element_type=jnp.float32)
+        proj, gram = (p, g) if x == 0 else (proj + p, gram + g)
+    part[:, 0:n_all] = proj
+    part[:, n_all:n_all + count] = gram / float(nx * n_row * ny * n_col)
+
+    share = count // n_row
+    own = pl.ds(pl.multiple_of(row * share, share), share)
+
+    def exchange(peers, axis, src_of, dst, sends, recvs):
+        result = []
+        for k, peer in enumerate(peers):
+            where = {"row": row, "col": col}
+            where[axis] = peer
+            result.append(pltpu.make_async_remote_copy(
+                src_ref=src_of(peer), dst_ref=dst, send_sem=sends.at[k], recv_sem=recvs.at[k],
+                device_id=where, device_id_type=pl.DeviceIdType.MESH))
+        for copy in result:
+            copy.start()
+        for copy in result:
+            copy.wait()
+
+    row_sums[row] = part[own, :]
+    exchange(
+        row_peers, "row", lambda peer: part.at[pl.ds(pl.multiple_of(peer * share, share), share)],
+        row_sums.at[row], sum_send, sum_recv)
+    value = row_sums[0]
+    for k in range(1, n_row):
+        value = value + row_sums[k]
+    col_sums[col] = value
+    exchange(col_peers, "col", lambda peer: col_sums.at[col], col_sums.at[col], col_send, col_recv)
+    value = col_sums[0]
+    for k in range(1, n_col):
+        value = value + col_sums[k]
+    total[own, :] = value
+    exchange(row_peers, "row", lambda peer: total.at[own], total.at[own], back_send, back_recv)
+    proj_out[...] = total[:, 0:n_all]
+    gram_out[...] = total[:, n_all:n_all + count]
     store_e.wait()
     store_h.wait()
 
 
-def run_steps(e_field, h_field, e_coef, pml_width):
+def shards(e_field, h_field, e_coef, basis, pml_width, snap_index):
     nz, nx, ny = e_coef.shape
     n_row, n_col = lax.axis_size("row"), lax.axis_size("col")
+    modes, count = basis.shape[0] * n_row, snap_index.shape[0]
     f32 = jnp.float32
+    wide = modes + (count + 127) // 128 * 128
     any_space = pl.BlockSpec(memory_space=pl.ANY)
+    smem, vmem = pl.BlockSpec(memory_space=pltpu.SMEM), pl.BlockSpec(memory_space=pltpu.VMEM)
     return pl.pallas_call(
         functools.partial(step_kernel, n_row, n_col),
-        out_shape=[jax.ShapeDtypeStruct(e_field.shape, f32)] * 2,
-        in_specs=[pl.BlockSpec(memory_space=pltpu.SMEM), any_space, any_space, any_space],
-        out_specs=[any_space, any_space],
+        out_shape=[
+            jax.ShapeDtypeStruct(e_field.shape, f32), jax.ShapeDtypeStruct(h_field.shape, f32),
+            jax.ShapeDtypeStruct((count, modes), f32), jax.ShapeDtypeStruct((count, count), f32),
+        ],
+        in_specs=[smem, smem, any_space, any_space, any_space, any_space],
+        out_specs=[any_space, any_space, vmem, vmem],
         scratch_shapes=[
-            pltpu.VMEM((3, nz + 1, nx, ny), f32), pltpu.VMEM((3, nz + 1, nx, ny), f32),
+            pltpu.VMEM((6, nz + 1, nx, ny), f32),
             pltpu.VMEM((nz, nx, ny), f32), pltpu.VMEM((8, nz, nx, ny), f32),
             pltpu.VMEM((2, nz, ny), f32), pltpu.VMEM((3, nz, ny), f32), pltpu.VMEM((2, nz, ny), f32),
             pltpu.VMEM((nx, ny), f32), pltpu.VMEM((2, nx, ny), f32), pltpu.VMEM((nx, ny), f32),
@@ -344,32 +445,21 @@
             pltpu.VMEM((2, nx, ny), f32), pltpu.VMEM((2, nx, ny), f32),
             pltpu.VMEM((nx, ny), f32), pltpu.VMEM((2, nx, ny), f32),
             pltpu.VMEM((12, nx, ny), f32),
-            pltpu.SemaphoreType.DMA((3,)),
+            pltpu.VMEM((modes * nx, ny), f32), pltpu.VMEM((count * nx, ny), f32),
+            pltpu.VMEM((count, wide), f32), pltpu.VMEM((n_row, count // n_row, wide), f32),
+            pltpu.VMEM((n_col, count // n_row, wide), f32), pltpu.VMEM((count, wide), f32),
+            pltpu.SemaphoreType.DMA((4,)),
             pltpu.SemaphoreType.DMA((6, 2)), pltpu.SemaphoreType.DMA((6, 2)),
             pltpu.SemaphoreType.DMA((2,)), pltpu.SemaphoreType.DMA((2,)),
+            pltpu.SemaphoreType.DMA((n_row - 1, STEPS)), pltpu.SemaphoreType.DMA((n_row - 1, STEPS)),
+            pltpu.SemaphoreType.DMA((n_row - 1,)), pltpu.SemaphoreType.DMA((n_row - 1,)),
+            pltpu.SemaphoreType.DMA((n_col - 1,)), pltpu.SemaphoreType.DMA((n_col - 1,)),
+            pltpu.SemaphoreType.DMA((n_row - 1,)), pltpu.SemaphoreType.DMA((n_row - 1,)),
         ],
         compiler_params=pltpu.CompilerParams(
             collective_id=0, has_side_effects=True, vmem_limit_bytes=32 * 1024 * 1024
         ),
-    )(pml_width, e_field, h_field, e_coef)
-
-
-def shards(e_field, h_field, e_coef, basis, pml_width, snap_index):
-    depth_z, rows_here, cols_here = e_coef.shape
-    full_x = rows_here * lax.axis_size("row")
-    full_y = cols_here * lax.axis_size("col")
-    e_field, h_field = run_steps(e_field, h_field, e_coef, pml_width)
-    planes = jnp.concatenate((e_field, h_field), 0).reshape(6 * depth_z, rows_here, cols_here)
-    snaps = jnp.take(planes, snap_index, axis=0)
-    count = snaps.shape[0]
-    flat = snaps.reshape(count, rows_here * cols_here)
-    gram_part = jnp.dot(flat, flat.T, precision=lax.Precision.HIGHEST) / float(full_x * full_y)
-    local_modes = lax.all_to_all(basis, "row", split_axis=1, concat_axis=0, tiled=True)
-    coef_part = jnp.dot(
-        flat, local_modes.reshape(local_modes.shape[0], -1).T, precision=lax.Precision.HIGHEST
-    )
-    coefficients, gram = lax.psum((coef_part, gram_part), ("row", "col"))
-    return (e_field, h_field, coefficients, gram)
+    )(pml_width, snap_index, e_field, h_field, e_coef, basis)
 
 
 def solution(mesh):

time: 131 us -> 87.6 us (0.67)
  blocking collectives: 39.9 us -> 0 us
  starting transfers between devices: 5.19 us -> 0 us
  local copies, waits for them, and re-layouts: 6.03 us -> 8.55 us
    psum x1 -> x0, blocking collectives: 39.9 us -> none  [shards(): coefficients, gram = lax.psum((coef_part, gram_part), ('row', 'col'))]
    all_to_all x1 -> x0, starting transfers between devices: 5.19 us -> none  [shards(): lax.all_to_all(basis, 'row', split_axis=1, concat_axis=0, tiled=True)]
    unnamed x13 -> x16, local copies, waits for them, and re-layouts: 4.05 us -> 8.55 us
    all_to_all x1 -> x0, local copies, waits for them, and re-layouts: 1.35 us -> none  [shards(): lax.all_to_all(basis, 'row', split_axis=1, concat_axis=0, tiled=True)]
  transfers between devices with their start and end apart: 1 -> 0, of which waited for: 0 -> 0; matrix products, arithmetic and copies ran while one was open for 1% -> 0% of each run, Pallas kernels for 59% -> 0%
where the time goes in v2:
time: 87.6 us; the launch traced here: 87.3 us
  Pallas kernels  78.1 us (89%)
  local copies, waits for them, and re-layouts  8.55 us (10%)
    pallas_call x1, Pallas kernels, shards(): pl.pallas_call(functools.partial(step_kernel, n_row, n_col), out_shape=[j...  78.1 us
    unnamed x16, local copies, waits for them, and re-layouts  8.55 us

profile of v2, /device:TPU:0, one launch (start us, length us, event | category | flops | bytes accessed | tf_op | source)
XLA Modules:
  0.0 87.3 jit_solution(4427348472499413471)
XLA Ops:
  0.6 0.0 copy-start
  0.6 1.1 %copy-done = f32[3,64,8,128]{3,2,1,0:T(8,128)S(1)} copy-done((f32[3,64,8,128]{3,2,1,0:T(8,128)S(1)}, f32[3,64,8,128]{3,2,1,0:T(8,128)}, u32[]{:S(2)}) %copy-start) | copy-done | bytes 786456
  1.8 0.0 copy-start.1
  1.8 1.1 %copy-done.1 = f32[3,64,8,128]{3,2,1,0:T(8,128)S(1)} copy-done((f32[3,64,8,128]{3,2,1,0:T(8,128)S(1)}, f32[3,64,8,128]{3,2,1,0:T(8,128)}, u32[]{:S(2)}) %copy-start.1) | copy-done | bytes 786456
  2.9 0.0 copy-start.2
  2.9 1.0 %copy-done.2 = f32[32,32,128]{2,1,0:T(8,128)S(1)} copy-done((f32[32,32,128]{2,1,0:T(8,128)S(1)}, f32[32,32,128]{2,1,0:T(8,128)}, u32[]{:S(2)}) %copy-start.2) | copy-done | bytes 524312
  3.9 0.0 copy-start.3
  3.9 0.9 %copy-done.3 = f32[64,8,128]{2,1,0:T(8,128)S(1)} copy-done((f32[64,8,128]{2,1,0:T(8,128)S(1)}, f32[64,8,128]{2,1,0:T(8,128)}, u32[]{:S(2)}) %copy-start.3) | copy-done | bytes 262168
  4.9 0.0 copy-start.4
  4.9 0.7 copy-done.4
  5.5 0.0 copy-start.5
  5.6 0.7 copy-done.5
  6.2 78.1 %shard_map.93 = (f32[3,64,8,128]{3,2,1,0:T(8,128)S(1)}, f32[3,64,8,128]{3,2,1,0:T(8,128)S(1)}, f32[64,128]{1,0:T(8,128)S(1)}, f32[64,64]{1,0:T(8,128)S(1)}) custom-call(s32[4]{0:T(128)S(1)} %copy-done.4, s32[64]{0:T(128)S(1)} %copy-done.5, f32[3,64,8,128]{3,2,1,0:T(8,128)S(1)} %copy-done, f32[3,64,8,128]{3,2,1,0:T(8,128)S(1)} %copy-done.1, ...), custom_call_target="tpu_custom_call" | custom-call | tf_op jit(solution)/shard_map/pallas_call | solution.py:429
  84.3 0.9 %copy.14 = f32[3,64,8,128]{3,2,1,0:T(8,128)} copy(f32[3,64,8,128]{3,2,1,0:T(8,128)S(1)} %get-tuple-element.8) | data formatting | bytes 1572864
  85.2 0.9 %copy.15 = f32[3,64,8,128]{3,2,1,0:T(8,128)} copy(f32[3,64,8,128]{3,2,1,0:T(8,128)S(1)} %get-tuple-element.9) | data formatting | bytes 1572864
  86.1 0.6 copy.16
  86.7 0.6 copy.17
Async XLA Ops:
  0.6 1.1 %copy-start = (f32[3,64,8,128]{3,2,1,0:T(8,128)S(1)}, f32[3,64,8,128]{3,2,1,0:T(8,128)}, u32[]{:S(2)}) copy-start(f32[3,64,8,128]{3,2,1,0:T(8,128)} %e_in.1) | copy-start | bytes 2359300
  1.8 1.1 %copy-start.1 = (f32[3,64,8,128]{3,2,1,0:T(8,128)S(1)}, f32[3,64,8,128]{3,2,1,0:T(8,128)}, u32[]{:S(2)}) copy-start(f32[3,64,8,128]{3,2,1,0:T(8,128)} %h_in.1) | copy-start | bytes 2359300
  2.9 1.0 %copy-start.2 = (f32[32,32,128]{2,1,0:T(8,128)S(1)}, f32[32,32,128]{2,1,0:T(8,128)}, u32[]{:S(2)}) copy-start(f32[32,32,128]{2,1,0:T(8,128)} %basis_in.1) | copy-start | bytes 1572868
  3.9 0.9 %copy-start.3 = (f32[64,8,128]{2,1,0:T(8,128)S(1)}, f32[64,8,128]{2,1,0:T(8,128)}, u32[]{:S(2)}) copy-start(f32[64,8,128]{2,1,0:T(8,128)} %coef_in.1) | copy-start | bytes 786436
  4.9 0.7 copy-start.4
  5.5 0.7 copy-start.5

commit v3 on v2

--- a/solution.py
+++ b/solution.py
@@ -29,7 +29,7 @@
     fields, coef_s, psi, first_x, last_x, h_last_x, first_y, last_y, h_last_y,
     next_x, prev_x, halo_x, halo_psi_x, next_y, prev_y, corner_x, corner_y, halo_y, halo_psi_y,
     prof, modes, snaps, part, row_sums, col_sums, total,
-    local_sem, send_sem, recv_sem, once_send, once_recv, mode_send, mode_recv,
+    local_sem, x_send, x_recv, send_sem, recv_sem, once_send, once_recv, mode_send, mode_recv,
     sum_send, sum_recv, col_send, col_recv, back_send, back_recv,
 ):
     e_s, h_s = fields.at[pl.ds(0, 3)], fields.at[pl.ds(3, 3)]
@@ -43,7 +43,10 @@
         (up, {"row": row - 1, "col": col}), (down, {"row": row + 1, "col": col}),
         (left, {"row": row, "col": col - 1}), (sw, {"row": row + 1, "col": col - 1}),
         (right, {"row": row, "col": col + 1}), (ne, {"row": row - 1, "col": col + 1}),
+        (left, {"row": row, "col": col - 1}),
     )
+    chunks = nz // UNROLL
+    half = chunks // 2
 
     load_e = pltpu.make_async_copy(e_in, e_s.at[:, pl.ds(0, nz)], local_sem.at[0])
     load_h = pltpu.make_async_copy(h_in, h_s.at[:, pl.ds(1, nz)], local_sem.at[1])
@@ -131,46 +134,44 @@
         return first, last0, last1
 
     def keep(cols):
-        first_y[...] = cols[0]
+        first_y[1] = cols[0]
         last_y[0] = pltpu.roll(cols[1], 1, 1)
         last_y[1] = pltpu.roll(cols[2], 1, 1)
 
-    def copies(slot):
-        parts = (
-            (first_x, next_x.at[slot]),
-            (last_x, prev_x.at[slot, :, pl.ds(0, nz)]),
-            (first_y, next_y.at[slot]),
-            (first_y, corner_x.at[slot]),
-            (last_y, prev_y.at[slot]),
-            (last_y.at[1], corner_y.at[slot]),
-        )
-        return [
-            pltpu.make_async_remote_copy(
-                src_ref=src, dst_ref=dst, send_sem=send_sem.at[m, slot], recv_sem=recv_sem.at[m, slot],
-                device_id=routes[m][1], device_id_type=pl.DeviceIdType.MESH)
-            for m, (src, dst) in enumerate(parts)
-        ]
-
-    def start_all(slot):
-        for m, copy in enumerate(copies(slot)):
-            @pl.when(routes[m][0])
-            def _():
-                copy.start()
-
-    arrives = (down, up, right, ne, left, sw)
-
-    def wait_recv(slot, which):
-        every = copies(slot)
-        for m in which:
-            @pl.when(arrives[m])
-            def _():
-                every[m].wait_recv()
-
-    def wait_send(slot):
-        for m, copy in enumerate(copies(slot)):
-            @pl.when(routes[m][0])
-            def _():
-                copy.wait_send()
+    def remote(m, src, dst, send, recv):
+        return pltpu.make_async_remote_copy(
+            src_ref=src, dst_ref=dst, send_sem=send, recv_sem=recv,
+            device_id=routes[m][1], device_id_type=pl.DeviceIdType.MESH)
+
+    def copy_of(m, slot, k=None):
+        if m < 2:
+            here = pl.ds(pl.multiple_of(k * UNROLL, UNROLL), UNROLL)
+            src, dst = ((first_x, next_x), (last_x, prev_x))[m]
+            return remote(
+                m, src.at[:, here], dst.at[slot, :, here], x_send.at[m, slot, k], x_recv.at[m, slot, k])
+        src, dst = {
+            2: (first_y.at[1], next_y.at[slot, 1]), 3: (first_y.at[1], corner_x.at[slot]),
+            4: (last_y, prev_y.at[slot]), 5: (last_y.at[1], corner_y.at[slot]),
+            6: (first_y.at[0], next_y.at[slot, 0]),
+        }[m]
+        return remote(m, src, dst, send_sem.at[m, slot], recv_sem.at[m, slot])
+
+    def start(m, slot, k=None):
+        @pl.when(routes[m][0])
+        def _():
+            copy_of(m, slot, k).start()
+
+    arrives = (down, up, right, ne, left, sw, right)
+
+    def wait_recv(m, slot, k=None):
+        @pl.when(arrives[m])
+        def _():
+            copy_of(m, slot, k).wait_recv()
+
+    def wait_send(m, slot, k=None):
+        @pl.when(routes[m][0])
+        def _():
+            copy_of(m, slot, k).wait_send()
 
     load_e.wait()
     load_h.wait()
@@ -189,6 +190,7 @@
 
     cols, hcol = lax.fori_loop(0, nz // UNROLL, first_pack, ((zero, zero, zero), zero))
     keep(cols)
+    first_y[0] = cols[0]
     h_last_y[...] = hcol
 
     count = n_row - 1 + n_col - 1 + sw.astype(jnp.int32) + ne.astype(jnp.int32)
@@ -199,7 +201,11 @@
             device_id=routes[m][1], device_id_type=pl.DeviceIdType.MESH)
         for k, (src, dst, m) in enumerate(((h_last_x, halo_x, 1), (h_last_y, halo_y, 4)))
     ]
-    start_all(0)
+    for k in range(chunks):
+        start(0, 0, k)
+        start(1, 0, k)
+    for m in (2, 4, 6, 3, 5):
+        start(m, 0)
     for k, m in enumerate((1, 4)):
         @pl.when(routes[m][0])
         def _():
@@ -219,9 +225,19 @@
 
     def magnetic(slot):
         hdx, hgx, hdy, hgy = prof[0], prof[1], prof[2], prof[3]
-        edge = next_y[slot]
 
         def body(k, carry):
+            wait_recv(0, slot, k)
+
+            @pl.when(k == 0)
+            def _():
+                wait_recv(6, slot)
+
+            @pl.when(k == half)
+            def _():
+                wait_recv(2, slot)
+
+            edge = next_y[slot, k // half]
             for j in range(UNROLL):
                 z = k * UNROLL + j
                 ex, ey, ez = e_s[0, z], e_s[1, z], e_s[2, z]
@@ -271,7 +287,7 @@
         hdx, hgx = prof[0], prof[1]
         hdy, hgy = prof[10], prof[11]
         ey = prev_y[slot, 1]
-        dy = first_y[...] - prev_y[slot, 0]
+        dy = first_y[1] - prev_y[slot, 0]
         below = jnp.broadcast_to(corner_y[slot, 0:1, :], (nx, ny))
         ey_dx = jnp.where(sub == nx - 1, below, pltpu.roll(ey, nx - 1, 0)) - ey
         ey_dz = pltpu.roll(pltpu.roll(ey, ny - 1, 1) - ey, nz, 1)
@@ -282,7 +298,7 @@
         change = jnp.where(lane < nz, ey_dx + px - dy - py, dy + py - ey_dz)
         halo_y[...] = mask * (halo_y[...] - time_step * change)
 
-    def electric():
+    def electric(s, slot):
         edx, egx, edy, egy = prof[4], prof[5], prof[6], prof[7]
         edge = halo_y[...]
 
@@ -311,6 +327,21 @@
                 ez = e_s[2, z] + amount * (hy_dx + p2 - hx_dy - p3)
                 e_s[0, z], e_s[1, z], e_s[2, z] = ex, ey, ez
                 cols = pack(z, ex, ey, ez, cols)
+            more = s < STEPS - 1
+
+            @pl.when(more)
+            def _():
+                start(0, slot, k)
+                start(1, slot, k)
+
+            @pl.when(k == half - 1)
+            def _():
+                first_y[0] = cols[0]
+
+                @pl.when(more)
+                def _():
+                    start(6, slot)
+
             return cols
 
         keep(lax.fori_loop(0, nz // UNROLL, body, (zero, zero, zero)))
@@ -319,9 +350,10 @@
         slot = lax.rem(s, 2)
         for copy in mode_copies(s):
             copy.start()
-        wait_recv(slot, (0, 2))
         magnetic(slot)
-        wait_recv(slot, (1, 3))
+        for k in range(chunks):
+            wait_recv(1, slot, k)
+        wait_recv(3, slot)
 
         @pl.when(s == 0)
         def _():
@@ -331,14 +363,20 @@
                     once[k].wait_recv()
 
         magnetic_row_before(slot)
-        wait_recv(slot, (4, 5))
+        wait_recv(4, slot)
+        wait_recv(5, slot)
         magnetic_column_before(slot)
-        wait_send(slot)
-        electric()
+        for k in range(chunks):
+            wait_send(0, slot, k)
+            wait_send(1, slot, k)
+        for m in range(2, 7):
+            wait_send(m, slot)
+        electric(s, 1 - slot)
 
         @pl.when(s < STEPS - 1)
         def _():
-            start_all(1 - slot)
+            for m in (2, 4, 3, 5):
+                start(m, 1 - slot)
 
         return carry
 
@@ -438,10 +476,10 @@
             pltpu.VMEM((6, nz + 1, nx, ny), f32),
             pltpu.VMEM((nz, nx, ny), f32), pltpu.VMEM((8, nz, nx, ny), f32),
             pltpu.VMEM((2, nz, ny), f32), pltpu.VMEM((3, nz, ny), f32), pltpu.VMEM((2, nz, ny), f32),
-            pltpu.VMEM((nx, ny), f32), pltpu.VMEM((2, nx, ny), f32), pltpu.VMEM((nx, ny), f32),
+            pltpu.VMEM((2, nx, ny), f32), pltpu.VMEM((2, nx, ny), f32), pltpu.VMEM((nx, ny), f32),
             pltpu.VMEM((2, 2, nz, ny), f32), pltpu.VMEM((2, 3, nz + 8, ny), f32),
             pltpu.VMEM((2, nz, ny), f32), pltpu.VMEM((3, nz, ny), f32),
-            pltpu.VMEM((2, nx, ny), f32), pltpu.VMEM((2, 2, nx, ny), f32),
+            pltpu.VMEM((2, 2, nx, ny), f32), pltpu.VMEM((2, 2, nx, ny), f32),
             pltpu.VMEM((2, nx, ny), f32), pltpu.VMEM((2, nx, ny), f32),
             pltpu.VMEM((nx, ny), f32), pltpu.VMEM((2, nx, ny), f32),
             pltpu.VMEM((12, nx, ny), f32),
@@ -449,7 +487,8 @@
             pltpu.VMEM((count, wide), f32), pltpu.VMEM((n_row, count // n_row, wide), f32),
             pltpu.VMEM((n_col, count // n_row, wide), f32), pltpu.VMEM((count, wide), f32),
             pltpu.SemaphoreType.DMA((4,)),
-            pltpu.SemaphoreType.DMA((6, 2)), pltpu.SemaphoreType.DMA((6, 2)),
+            pltpu.SemaphoreType.DMA((2, 2, nz // UNROLL)), pltpu.SemaphoreType.DMA((2, 2, nz // UNROLL)),
+            pltpu.SemaphoreType.DMA((7, 2)), pltpu.SemaphoreType.DMA((7, 2)),
             pltpu.SemaphoreType.DMA((2,)), pltpu.SemaphoreType.DMA((2,)),
             pltpu.SemaphoreType.DMA((n_row - 1, STEPS)), pltpu.SemaphoreType.DMA((n_row - 1, STEPS)),
             pltpu.SemaphoreType.DMA((n_row - 1,)), pltpu.SemaphoreType.DMA((n_row - 1,)),
@@ -457,7 +496,7 @@
             pltpu.SemaphoreType.DMA((n_row - 1,)), pltpu.SemaphoreType.DMA((n_row - 1,)),
         ],
         compiler_params=pltpu.CompilerParams(
-            collective_id=0, has_side_effects=True, vmem_limit_bytes=32 * 1024 * 1024
+            collective_id=0, has_side_effects=True, vmem_limit_bytes=67_043_328
         ),
     )(pml_width, snap_index, e_field, h_field, e_coef, basis)
 

time: 87.6 us -> 77.5 us (0.88)
  Pallas kernels: 78.1 us -> 72.2 us
  local copies, waits for them, and re-layouts: 8.55 us -> 4.41 us
    pallas_call x1, Pallas kernels: 78.1 us -> 72.2 us  [shards(): pl.pallas_call(functools.partial(step_kernel, n_row, n_col), out_shape=[j...]
    unnamed x16 -> x10, local copies, waits for them, and re-layouts: 8.55 us -> 4.41 us
where the time goes in v3:
time: 77.5 us; the launch traced here: 77.3 us
  Pallas kernels  72.2 us (93%)
  local copies, waits for them, and re-layouts  4.41 us (6%)
    pallas_call x1, Pallas kernels, shards(): pl.pallas_call(functools.partial(step_kernel, n_row, n_col), out_shape=[j...  72.2 us
    unnamed x10, local copies, waits for them, and re-layouts  4.41 us

profile of v3, /device:TPU:0, one launch (start us, length us, event | category | flops | bytes accessed | tf_op | source)
XLA Modules:
  0.0 77.3 jit_solution(11039718100704408739)
XLA Ops:
  0.6 72.2 %shard_map.93 = (f32[3,64,8,128]{3,2,1,0:T(8,128)}, f32[3,64,8,128]{3,2,1,0:T(8,128)}, f32[64,128]{1,0:T(8,128)}, f32[64,64]{1,0:T(8,128)}) custom-call(s32[4]{0:T(128)} %width_ref.1, s32[64]{0:T(128)} %index_ref.1, f32[3,64,8,128]{3,2,1,0:T(8,128)} %e_in.1, f32[3,64,8,128]{3,2,1,0:T(8,128)} %h_in.1, f32[64,8,128]{2,1,0:T(8,128)} %coef_in.1, ...), custom_call_target="tpu_custom_call" | custom-call | tf_op jit(solution)/shard_map/pallas_call | solution.py:467
  72.8 0.0 copy-start
  72.8 2.1 %copy.14 = f32[3,64,8,128]{3,2,1,0:T(8,128)} copy(f32[3,64,8,128]{3,2,1,0:T(8,128)} %get-tuple-element.8) | data formatting | bytes 1572864
  75.0 0.0 copy-done
  75.0 0.0 copy-start.2
  75.0 0.9 %copy.15 = f32[3,64,8,128]{3,2,1,0:T(8,128)} copy(f32[3,64,8,128]{3,2,1,0:T(8,128)S(1)} %copy-done) | data formatting | bytes 1572864
  75.9 0.0 copy-done.2
  75.9 0.0 copy-start.1
  75.9 0.6 copy.16
  76.5 0.2 copy-done.1
  76.6 0.6 copy.17
Async XLA Ops:
  72.8 2.1 %copy-start = (f32[3,64,8,128]{3,2,1,0:T(8,128)S(1)}, f32[3,64,8,128]{3,2,1,0:T(8,128)}, u32[]{:S(2)}) copy-start(f32[3,64,8,128]{3,2,1,0:T(8,128)} %get-tuple-element.9) | copy-start | bytes 2359300
  75.0 0.9 %copy-start.2 = (f32[64,128]{1,0:T(8,128)S(1)}, f32[64,128]{1,0:T(8,128)}, u32[]{:S(2)}) copy-start(f32[64,128]{1,0:T(8,128)} %get-tuple-element.10) | copy-start | bytes 98308
  75.9 0.8 copy-start.1

commit v4 on v3

--- a/solution.py
+++ b/solution.py
@@ -393,13 +393,16 @@
     count = snaps.shape[0] // nx
 
     def pick(s, carry):
-        index = index_ref[s]
-        c = index // nz
-        z = index - c * nz + (c // 3)
-        snaps[pl.ds(pl.multiple_of(s * nx, nx), nx), :] = fields[c, z]
+        planes = []
+        for j in range(8):
+            index = index_ref[s * 8 + j]
+            c = index // nz
+            planes.append(fields[c, index - c * nz + (c // 3)])
+        for j in range(8):
+            snaps[pl.ds(pl.multiple_of((s * 8 + j) * nx, nx), nx), :] = planes[j]
         return carry
 
-    lax.fori_loop(0, count, pick, 0)
+    lax.fori_loop(0, count // 8, pick, 0)
     load_b.wait()
 
     def wait_modes(s, carry):

time: 77.5 us -> 76.9 us (level)
  no operation moved by 1% of the time
where the time goes in v4:
time: 76.9 us; the launch traced here: 76.6 us
  Pallas kernels  71.6 us (93%)
  local copies, waits for them, and re-layouts  4.41 us (6%)
    pallas_call x1, Pallas kernels, shards(): pl.pallas_call(functools.partial(step_kernel, n_row, n_col), out_shape=[j...  71.6 us
    unnamed x10, local copies, waits for them, and re-layouts  4.41 us

profile of v4, /device:TPU:0, one launch (start us, length us, event | category | flops | bytes accessed | tf_op | source)
XLA Modules:
  0.0 76.6 jit_solution(6170011844363688621)
XLA Ops:
  0.6 71.6 %shard_map.93 = (f32[3,64,8,128]{3,2,1,0:T(8,128)}, f32[3,64,8,128]{3,2,1,0:T(8,128)}, f32[64,128]{1,0:T(8,128)}, f32[64,64]{1,0:T(8,128)}) custom-call(s32[4]{0:T(128)} %width_ref.1, s32[64]{0:T(128)} %index_ref.1, f32[3,64,8,128]{3,2,1,0:T(8,128)} %e_in.1, f32[3,64,8,128]{3,2,1,0:T(8,128)} %h_in.1, f32[64,8,128]{2,1,0:T(8,128)} %coef_in.1, ...), custom_call_target="tpu_custom_call" | custom-call | tf_op jit(solution)/shard_map/pallas_call | solution.py:470
  72.2 0.0 copy-start
  72.2 2.1 %copy.14 = f32[3,64,8,128]{3,2,1,0:T(8,128)} copy(f32[3,64,8,128]{3,2,1,0:T(8,128)} %get-tuple-element.8) | data formatting | bytes 1572864
  74.3 0.0 copy-done
  74.3 0.0 copy-start.2
  74.3 0.9 %copy.15 = f32[3,64,8,128]{3,2,1,0:T(8,128)} copy(f32[3,64,8,128]{3,2,1,0:T(8,128)S(1)} %copy-done) | data formatting | bytes 1572864
  75.2 0.0 copy-done.2
  75.2 0.0 copy-start.1
  75.2 0.6 copy.16
  75.8 0.2 copy-done.1
  76.0 0.6 copy.17
Async XLA Ops:
  72.2 2.1 %copy-start = (f32[3,64,8,128]{3,2,1,0:T(8,128)S(1)}, f32[3,64,8,128]{3,2,1,0:T(8,128)}, u32[]{:S(2)}) copy-start(f32[3,64,8,128]{3,2,1,0:T(8,128)} %get-tuple-element.9) | copy-start | bytes 2359300
  74.3 0.9 %copy-start.2 = (f32[64,128]{1,0:T(8,128)S(1)}, f32[64,128]{1,0:T(8,128)}, u32[]{:S(2)}) copy-start(f32[64,128]{1,0:T(8,128)} %get-tuple-element.10) | copy-start | bytes 98308
  75.2 0.8 %copy-start.1 = (f32[64,64]{1,0:T(8,128)S(1)}, f32[64,64]{1,0:T(8,128)}, u32[]{:S(2)}) copy-start(f32[64,64]{1,0:T(8,128)} %get-tuple-element.11) | copy-start | bytes 49156
